TPU v7x, 32 devices: a whole 2x2x4 slice. The times are simulated.
32 devices in a mesh: rep: 8 (over z, x), tp: 4 (over y, core).
Axes of the slice: x: 2, y: 2, z: 4, core: 2. Of those that a mesh axis runs over, the one named last changes fastest.
Arguments:
- tokens: bfloat16 [64, 4096], P(('rep', 'tp')), may hold values from -6 to 6
- conv_state: bfloat16 [3, 64, 8192], P(None, 'rep', 'tp'), may hold values from -6 to 6
- ssm_state: float32 [64, 16, 8192], P('rep', None, 'tp'), may hold values from -6 to 6
- norm_gains: bfloat16 [2, 4096], P(None, ('rep', 'tp')), may hold values from 0.5 to 1.5
- conv_weight: bfloat16 [4, 8192], P(None, ('rep', 'tp')), may hold values from -3 to 3
- conv_skip: bfloat16 [2, 8192], P(None, ('rep', 'tp')), may hold values from -3 to 3
- step_bias: bfloat16 [8192], P(('rep', 'tp')), may hold values from -5 to -1
- decay_log: bfloat16 [16, 8192], P(None, ('rep', 'tp')), may hold values from 0 to 2.796875
- input_proj: bfloat16 [4096, 2, 8192], P(('rep', 'tp')), may hold values from -0.09375 to 0.09375
- select_proj: bfloat16 [8192, 288], P('tp', 'rep'), may hold values from -0.0625 to 0.0625
- step_proj: bfloat16 [256, 8192], P(('rep', 'tp')), may hold values from -0.375 to 0.375
- output_proj: bfloat16 [8192, 4096], P(None, ('rep', 'tp')), may hold values from -0.0625 to 0.0625
- router: bfloat16 [4096, 16], P(('rep', 'tp')), may hold values from -0.09375 to 0.09375
- expert_proj: bfloat16 [4096, 2, 2, 12288], P(('rep', 'tp')), may hold values from -0.09375 to 0.09375
- expert_ids: int32 [64, 2], P(('rep', 'tp')), may hold values from 0 to 15, as said below
Outputs:
- mamba_out: bfloat16 [64, 4096], P(('rep', 'tp'))
- conv_next: bfloat16 [3, 64, 8192], P(None, 'rep', 'tp')
- ssm_next: float32 [64, 16, 8192], P('rep', None, 'tp')
- expert_hidden: bfloat16 [128, 12288], P('rep', 'tp')
Inputs may be any that keep to these rules, and one draw needn't show every extreme that they name: `expert_ids`: each row names two different experts. Within each aligned block of 2 rows (the rows of one device) each expert e < 2 is named by at most 2 rows.
All inputs are finite; a program needn't handle non-finite values.
Results may differ from a plain program's by a relative error of at most 0.04.
Values may be sent and summed in bfloat16 or wider, within the bound.
A program may use at most 192 MiB of HBM per device.

v0:
```python
import jax
import jax.numpy as jnp
from jax import lax
from jax.sharding import PartitionSpec as P

CAPACITY = 2


epsilon = 1e-05


def norm_scale(values, gain):
    mean_square = jnp.mean(values * values, axis=-1, keepdims=True)
    return values * lax.rsqrt(mean_square + epsilon) * gain.astype(jnp.float32)


def shards(
    tokens,
    conv_state,
    ssm_state,
    norm_gains,
    conv_weight,
    conv_skip,
    step_bias,
    decay_log,
    input_proj,
    select_proj,
    step_proj,
    output_proj,
    router,
    expert_proj,
    expert_ids,
):
    tp_count = lax.axis_size("tp")
    rep_count = lax.axis_size("rep")
    tp_index = lax.axis_index("tp")
    norm_gain, conv_taps, skip_rows, shift_full, decay_full, router_full = (
        lax.all_gather(norm_gains, ("rep", "tp"), axis=1, tiled=True),
        lax.all_gather(conv_weight, ("rep", "tp"), axis=1, tiled=True),
        lax.all_gather(conv_skip, ("rep", "tp"), axis=1, tiled=True),
        lax.all_gather(step_bias, ("rep", "tp"), axis=0, tiled=True),
        lax.all_gather(decay_log, ("rep", "tp"), axis=1, tiled=True),
        lax.all_gather(router, ("rep", "tp"), axis=0, tiled=True),
    )
    inner_dev = ssm_state.shape[2]
    channel_start = tp_index * inner_dev
    conv_taps = lax.dynamic_slice_in_dim(conv_taps, channel_start, inner_dev, 1).astype(jnp.float32)
    skip_rows = lax.dynamic_slice_in_dim(skip_rows, channel_start, inner_dev, 1).astype(jnp.float32)
    shift_dev = lax.dynamic_slice_in_dim(shift_full, channel_start, inner_dev, 0).astype(
        jnp.float32
    )
    decay_dev = lax.dynamic_slice_in_dim(decay_full, channel_start, inner_dev, 1).astype(
        jnp.float32
    )
    model_rows = input_proj.shape[0]
    inner_all = input_proj.shape[2]
    input_blocks, expert_blocks, step_blocks = (
        lax.all_to_all(
            input_proj.reshape(model_rows, 1, 2, inner_all),
            "tp",
            split_axis=3,
            concat_axis=0,
            tiled=True,
        ),
        lax.all_to_all(expert_proj, "tp", split_axis=3, concat_axis=0, tiled=True),
        lax.all_to_all(
            step_proj.reshape(step_proj.shape[0], 1, 1, inner_all),
            "tp",
            split_axis=3,
            concat_axis=0,
            tiled=True,
        ),
    )
    output_blocks = lax.all_to_all(output_proj, "tp", split_axis=0, concat_axis=1, tiled=True)
    residual_in = tokens.astype(jnp.float32)
    normed = norm_scale(residual_in, norm_gain[0]).astype(jnp.bfloat16)
    features = lax.all_gather(normed, "tp", axis=0, tiled=True)
    shard_piece = lax.all_gather(input_blocks, "rep", axis=0, tiled=True)
    piece_rows = shard_piece.shape[0]
    projected = jnp.dot(
        features, shard_piece.reshape(piece_rows, 2 * inner_dev), preferred_element_type=jnp.float32
    )
    output_rows, step_rows, select_rows = (
        lax.all_gather(output_blocks, "rep", axis=1, tiled=True),
        lax.all_gather(step_blocks, "rep", axis=0, tiled=True),
        lax.all_gather(select_proj, "rep", axis=1, tiled=True),
    )
    step_rows = step_rows.reshape(step_rows.shape[0], inner_dev)
    step_rank = step_rows.shape[0]
    state_count = ssm_state.shape[1]
    conv_input = projected[:, :inner_dev]
    gate_z = projected[:, inner_dev:]
    history = conv_state.astype(jnp.float32)
    conv_mix = (
        jnp.sum(conv_taps[:-1, None, :] * history, axis=0)
        + conv_taps[-1] * conv_input
        + skip_rows[0]
    )
    conv_next = jnp.concatenate([conv_state[1:], conv_input.astype(jnp.bfloat16)[None]], axis=0)
    activated = jax.nn.silu(conv_mix)
    select_part = jnp.dot(
        activated.astype(jnp.bfloat16), select_rows, preferred_element_type=jnp.float32
    )
    selected = lax.psum(select_part.astype(jnp.bfloat16), "tp").astype(jnp.float32)
    step_low = selected[:, :step_rank].astype(jnp.bfloat16)
    input_map = selected[:, step_rank : step_rank + state_count]
    output_map = selected[:, step_rank + state_count :]
    step_size = jax.nn.softplus(
        jnp.dot(step_low, step_rows, preferred_element_type=jnp.float32) + shift_dev
    )
    decay_rate = -jnp.exp(decay_dev)
    factor = jnp.exp(step_size[:, None, :] * decay_rate[None])
    ssm_next = factor * ssm_state + (step_size * activated)[:, None, :] * input_map[:, :, None]
    readout = jnp.sum(ssm_next * output_map[:, :, None], axis=1) + skip_rows[1] * activated
    gated_out = (readout * jax.nn.silu(gate_z)).astype(jnp.bfloat16)
    output_part = jnp.dot(gated_out, output_rows, preferred_element_type=jnp.float32)
    mixer_out = lax.psum_scatter(
        output_part.astype(jnp.bfloat16), "tp", scatter_dimension=0, tiled=True
    ).astype(jnp.float32)
    residual = residual_in + mixer_out
    mamba_out = residual.astype(jnp.bfloat16)
    moe_in = norm_scale(residual, norm_gain[1]).astype(jnp.bfloat16)
    logits = jnp.dot(moe_in, router_full, preferred_element_type=jnp.float32)
    expert_total = logits.shape[1]
    choose = (
        expert_ids[:, :, None] == jnp.arange(expert_total, dtype=jnp.int32)[None, None, :]
    ).astype(jnp.float32)
    picked = jnp.sum(choose * logits[:, None, :], axis=2)
    first_gate = jax.nn.sigmoid(picked[:, 0] - picked[:, 1])
    second_gate = jax.nn.sigmoid(picked[:, 1] - picked[:, 0])
    window_count = expert_blocks.shape[1]
    window = jnp.arange(window_count, dtype=jnp.int32)
    names_first = expert_ids[:, 0:1] == window[None, :]
    names_second = expert_ids[:, 1:2] == window[None, :]
    zero = jnp.zeros((), jnp.float32)
    gate_w = jnp.where(names_first, first_gate[:, None], zero) + jnp.where(
        names_second, second_gate[:, None], zero
    )
    routed = (names_first | names_second).astype(jnp.int32)
    position = jnp.cumsum(routed, axis=0) - routed
    slot_of = (position[:, :, None] == jnp.arange(CAPACITY, dtype=jnp.int32)[None, None, :]) & (
        routed[:, :, None] > 0
    )
    slot_x = jnp.einsum(
        "tec,td->ecd", slot_of.astype(jnp.bfloat16), moe_in, preferred_element_type=jnp.float32
    )
    slot_local = window_count * CAPACITY
    slot_x = slot_x.astype(jnp.bfloat16).reshape(slot_local, moe_in.shape[1])
    slot_gate = (
        jnp.einsum("tec,te->ec", slot_of.astype(jnp.float32), gate_w)
        .astype(jnp.bfloat16)
        .reshape(slot_local)
    )
    feature_rows = expert_blocks.shape[0]
    spread_slots = lax.all_to_all(slot_x, "rep", split_axis=1, concat_axis=0, tiled=True)
    gathered, gate_all = (
        lax.all_gather(spread_slots, "tp", axis=0, tiled=True),
        lax.all_gather(slot_gate, "tp", axis=0, tiled=True),
    )
    gathered = gathered.reshape(tp_count, rep_count, slot_local, feature_rows)
    gathered = gathered.transpose(1, 0, 2, 3).reshape(
        rep_count * tp_count * slot_local, feature_rows
    )
    hidden_dev = expert_blocks.shape[3]
    group_rows = tp_count * slot_local
    picked_rows = gathered
    picked_rows = picked_rows.reshape(
        lax.axis_size("rep") * group_rows // slot_local, window_count, CAPACITY, feature_rows
    )
    product = jnp.einsum(
        "gecd,dexf->gecxf", picked_rows, expert_blocks, preferred_element_type=jnp.float32
    )
    summed = lax.psum_scatter(
        product.reshape(lax.axis_size("rep") * group_rows, 2 * hidden_dev).astype(jnp.bfloat16),
        "rep",
        scatter_dimension=0,
        tiled=True,
    ).astype(jnp.float32)
    hidden = (
        gate_all.astype(jnp.float32)[:, None]
        * jax.nn.silu(summed[:, :hidden_dev])
        * summed[:, hidden_dev:]
    )
    expert_hidden = hidden.astype(jnp.bfloat16)
    return (mamba_out, conv_next, ssm_next, expert_hidden)


def solution(mesh):
    in_specs = (
        P(("rep", "tp"), None),
        P(None, "rep", "tp"),
        P("rep", None, "tp"),
        P(None, ("rep", "tp")),
        P(None, ("rep", "tp")),
        P(None, ("rep", "tp")),
        P(("rep", "tp")),
        P(None, ("rep", "tp")),
        P(("rep", "tp"), None, None),
        P("tp", "rep"),
        P(("rep", "tp"), None),
        P(None, ("rep", "tp")),
        P(("rep", "tp"), None),
        P(("rep", "tp"), None, None, None),
        P(("rep", "tp"), None),
    )
    out_specs = (P(("rep", "tp"), None), P(None, "rep", "tp"), P("rep", None, "tp"), P("rep", "tp"))
    return jax.shard_map(shards, mesh=mesh, in_specs=in_specs, out_specs=out_specs, check_vma=False)
```

profile of v0, /device:TPU:0, one launch (start us, length us, event | category | flops | bytes accessed | tf_op | source)
XLA Modules:
  0.0 1170.5 jit_solution(6443749965253223028)
XLA Ops:
  7.2 14.8 %copy.82 = bf16[128,2,8192]{0,1,2:T(2,128)(2,1)} copy(bf16[128,2,8192]{2,1,0:T(2,128)(2,1)} %param.23) | data formatting | bytes 8388608 | tf_op args[8]
  22.0 4.9 all-to-all-start
  26.9 0.7 all-gather.14.cloned.1.call-update
  27.6 48.1 %all-to-all-done = bf16[128,1,2,8192]{0,2,1,3:T(2,128)(2,1)} async-done(((bf16[128,1,2,8192]{0,2,1,3:T(2,128)(2,1)}), bf16[128,1,2,8192]{0,2,1,3:T(2,128)(2,1)}, u32[]{:S(2)}, u32[]{:S(2)}) %all-to-all-start) | async-done | bytes 4194336 | tf_op jit(solution)/shard_map/all_to_all | solution.py:58
  75.7 4.7 copy.83
  80.4 6.3 copy.84
  86.8 0.8 copy-done.3
  87.6 6.7 copy.86
  94.8 45.3 %reduce.9 = bf16[8192,8]{1,0:T(8,128)(2,1)S(1)} reduce(bf16[8192,1,1,8]{3,2,1,0:T(2,128)(2,1)} %bitcast.85, bf16[]{:T(256)} %broadcast.158), dimensions={1,2}, to_apply=%bitcast.66.reduce_sub_computation | reduce | bytes 262146
  140.0 2.2 reshape.227
  142.3 7.0 all_to_all.92
  149.2 5.9 reshape.228
  155.1 7.8 copy.87
  163.0 0.7 copy.102
  163.8 29.3 %all_to_all.93 = bf16[4,2048,128]{2,1,0:T(8,128)(2,1)S(1)} all-to-all(bf16[4,2048,128]{2,1,0:T(8,128)(2,1)} %bitcast.91), channel_id=1, replica_groups=mesh['rep'=8,'tp'=4] {'tp'}, dimensions={0} | all-to-all | bytes 4194304 | tf_op jit(solution)/shard_map/all_to_all | solution.py:74
  193.1 2.7 copy.89
  195.8 41.3 %copy.92 = bf16[128,2,2,12288]{0,2,1,3:T(2,128)(2,1)} copy(bf16[128,2,2,12288]{3,2,1,0:T(2,128)(2,1)} %param.28) | data formatting | bytes 25165824 | tf_op args[13]
  237.2 6.5 all-to-all-start.4
  243.7 179.3 %all_gather.39 = bf16[4,8192]{1,0:T(4,128)(2,1)S(1)} all-gather(bf16[4,256]{1,0:T(4,128)(2,1)S(1)} %copy-done.7), channel_id=1, replica_groups=mesh['rep'=8,'tp'=4] {'rep','tp'}, dimensions={1}, use_global_device_ids=true | all-gather | bytes 67584 | tf_op jit(solution)/shard_map/all_gather | solution.py:39
  423.0 49.8 %all_gather.40 = bf16[2,4096]{1,0:T(2,128)(2,1)S(1)} all-gather(bf16[2,128]{1,0:T(2,128)(2,1)S(1)} %copy-done.10), channel_id=1, replica_groups=mesh['rep'=8,'tp'=4] {'rep','tp'}, dimensions={1}, use_global_device_ids=true | all-gather | bytes 16896 | tf_op jit(solution)/shard_map/all_gather | solution.py:38
  473.1 5.4 all-gather
  478.6 42.1 %all-gather.2 = bf16[32,1,256]{2,1,0:T(2,128)(2,1)S(1)} all-gather(bf16[1,1,256]{2,1,0:T(2,128)(2,1)S(1)} %reshape.211), channel_id=1, replica_groups=mesh['rep'=8,'tp'=4] {'rep','tp'}, dimensions={0}, use_global_device_ids=true | all-gather | bytes 16896 | tf_op jit(solution)/shard_map/all_gather | solution.py:41
  521.2 50.8 %all_gather.43 = bf16[2,8192]{1,0:T(2,128)(2,1)S(1)} all-gather(bf16[2,256]{1,0:T(2,128)(2,1)S(1)} %copy-done.9), channel_id=1, replica_groups=mesh['rep'=8,'tp'=4] {'rep','tp'}, dimensions={1}, use_global_device_ids=true | all-gather | bytes 33792 | tf_op jit(solution)/shard_map/all_gather | solution.py:40
  572.0 54.9 %all_gather.47 = bf16[16,8192]{1,0:T(8,128)(2,1)S(1)} all-gather(bf16[16,256]{1,0:T(8,128)(2,1)S(1)} %copy-done.5), channel_id=1, replica_groups=mesh['rep'=8,'tp'=4] {'rep','tp'}, dimensions={1}, use_global_device_ids=true | all-gather | bytes 270336 | tf_op jit(solution)/shard_map/all_gather | solution.py:42
  627.0 1.4 reshape.210
  628.4 99.1 %all-gather.8.cloned.1.call-done = bf16[4096,1,2,2048]{3,0,2,1:T(8,128)(2,1)} async-done(((bf16[512,1,2,2048]{3,0,2,1:T(8,128)(2,1)}), bf16[4096,1,2,2048]{3,0,2,1:T(8,128)(2,1)}) %all-gather.8.cloned.1.call-update) | async-done | bytes 33554448 | tf_op jit(solution)/shard_map/all_gather | solution.py:78
  727.5 40.1 %copy.85 = bf16[4096,1,2,2048]{0,3,2,1:T(8,128)(2,1)} copy(bf16[4096,1,2,2048]{3,0,2,1:T(8,128)(2,1)} %all-gather.8.cloned.1.call-done) | data formatting | bytes 67108864 | tf_op jit(solution)/shard_map/all_gather | solution.py:78
  767.6 14.8 %fusion.31 = f32[8,4096]{1,0:T(8,128)S(1)} fusion(bf16[8,4096]{1,0:T(8,128)(2,1)S(1)} %reshape.208, bf16[4096,4096]{0,1:T(8,128)(2,1)} %bitcast.80), kind=kOutput, calls=%fused_computation.69 | convolution fusion | flops 268435456 | bytes 33751040 | tf_op jit(solution)/shard_map/dot_general | solution.py:80
  782.9 6.8 psum.7
  789.8 1.5 fusion.30
  791.3 1.5 multiply_reduce_fusion
  792.8 206.0 %all-gather.12.cloned.1.call-done = bf16[2048,4096]{0,1:T(8,128)(2,1)} async-done(((bf16[2048,512]{0,1:T(8,128)(2,1)}), bf16[2048,4096]{0,1:T(8,128)(2,1)}) %all-gather.12.cloned.1.call-update) | async-done | bytes 16777232 | tf_op jit(solution)/shard_map/all_gather | solution.py:84
  998.8 10.8 convolution_convert_fusion
  1011.0 28.6 %all-reduce.4.cloned.1.call-done = bf16[8,4096]{1,0:T(8,128)(2,1)} async-done(((bf16[8,4096]{1,0:T(8,128)(2,1)}), bf16[8,4096]{1,0:T(8,128)(2,1)}) %all-reduce.4.cloned.1.call-update) | async-done | bytes 65552
  1039.5 1.0 multiply_reduce_fusion.2
  1040.5 1.5 multiply_convert_fusion.2
  1042.8 5.5 all-to-all-start.3
  1048.4 31.2 %copy.93 = bf16[128,2,2,4,3072]{4,0,3,2,1:T(8,128)(2,1)} copy(bf16[128,2,2,4,3072]{0,2,1,4,3:T(2,128)(2,1)} %bitcast.30) | data formatting | bytes 25165824 | tf_op jit(solution)/shard_map/all_to_all | solution.py:65
  1079.6 5.6 all_gather.51
  1085.5 6.9 fusion
  1092.4 1.6 copy.94
  1094.0 1.5 copy.100
  1096.2 41.5 %all_gather.49 = bf16[4096,16]{0,1:T(8,128)(2,1)S(1)} all-gather(bf16[128,16]{0,1:T(8,128)(2,1)S(1)} %copy-done.6), channel_id=1, replica_groups=mesh['rep'=8,'tp'=4] {'rep','tp'}, dimensions={0}, use_global_device_ids=true | all-gather | bytes 135168 | tf_op jit(solution)/shard_map/all_gather | solution.py:43
  1138.7 0.7 pad_maximum_fusion
  1139.3 6.0 all-reduce
  1145.3 16.7 %reduce-scatter.2.cloned.1.call-done = bf16[16,6144]{1,0:T(8,128)(2,1)} async-done(((bf16[128,6144]{1,0:T(8,128)(2,1)}), bf16[16,6144]{1,0:T(8,128)(2,1)}) %reduce-scatter.2.cloned.1.call-update) | async-done | bytes 196624 | tf_op jit(solution)/shard_map/reduce_scatter | solution.py:173
  1162.0 1.0 convert_element_type.117
  1162.9 0.7 fusion.2
  (84 shorter events, 5.0 us)
Async XLA Ops:
  22.0 53.8 %all-to-all-start = ((bf16[128,1,2,8192]{0,2,1,3:T(2,128)(2,1)}), bf16[128,1,2,8192]{0,2,1,3:T(2,128)(2,1)}, u32[]{:S(2)}, u32[]{:S(2)}) async-start(bf16[128,1,2,8192]{0,2,1,3:T(2,128)(2,1)} %bitcast.83), calls=%async_computation | async-start | bytes 8388608 | tf_op jit(solution)/shard_map/all_to_all | solution.py:58
  26.8 600.2 %all-gather.14.cloned.1.call-start = ((), (), s32[]{:S(2)}) async-start(), calls=%async_computation.10 | async-start | bytes 1474560 | tf_op jit(solution)/shard_map/all_gather | solution.py:86
  27.6 700.0 %all-gather.8.cloned.1.call-start = ((), (), s32[]{:S(2)}) async-start(), calls=%async_computation.6 | async-start | bytes 37748736 | tf_op jit(solution)/shard_map/all_gather | solution.py:78
  86.7 0.9 copy-start.3
  86.7 703.1 %all-gather.10.cloned.1.call-start = ((), (), s32[]{:S(2)}) async-start(), calls=%async_computation.7 | async-start | bytes 1179648 | tf_op jit(solution)/shard_map/all_gather | solution.py:85
  163.8 835.0 %all-gather.12.cloned.1.call-start = ((), (), s32[]{:S(2)}) async-start(), calls=%async_computation.8 | async-start | bytes 18874368 | tf_op jit(solution)/shard_map/all_gather | solution.py:84
  237.1 6.6 copy-start.7
  237.1 185.9 %copy-start.10 = (bf16[2,128]{1,0:T(2,128)(2,1)S(1)}, bf16[2,128]{1,0:T(2,128)(2,1)}, u32[]{:S(2)}) copy-start(bf16[2,128]{1,0:T(2,128)(2,1)} %param.18) | copy-start | bytes 1540
  237.1 235.7 %copy-start.2 = (bf16[2,4096]{1,0:T(2,128)(2,1)S(1)}, bf16[2,4096]{1,0:T(2,128)(2,1)}, u32[]{:S(2)}) copy-start(bf16[2,4096]{1,0:T(2,128)(2,1)} %param.15) | copy-start | bytes 49156
  237.1 241.4 %copy-start.11 = (bf16[256]{0:T(256)(128)(2,1)S(1)}, bf16[256]{0:T(256)(128)(2,1)}, u32[]{:S(2)}) copy-start(bf16[256]{0:T(256)(128)(2,1)} %param.21) | copy-start | bytes 1540
  237.1 283.6 %copy-start.4 = (s32[2,2]{1,0:T(2,128)S(1)}, s32[2,2]{1,0:T(2,128)}, u32[]{:S(2)}) copy-start(s32[2,2]{1,0:T(2,128)} %param.29) | copy-start | bytes 52
  237.2 284.0 %copy-start.9 = (bf16[2,256]{1,0:T(2,128)(2,1)S(1)}, bf16[2,256]{1,0:T(2,128)(2,1)}, u32[]{:S(2)}) copy-start(bf16[2,256]{1,0:T(2,128)(2,1)} %param.20) | copy-start | bytes 3076
  237.2 334.8 %copy-start.1 = (bf16[3,8,2048]{2,1,0:T(8,128)(2,1)S(1)}, bf16[3,8,2048]{2,1,0:T(8,128)(2,1)}, u32[]{:S(2)}) copy-start(bf16[3,8,2048]{2,1,0:T(8,128)(2,1)} %param.16) | copy-start | bytes 294916
  237.2 334.8 %copy-start.5 = (bf16[16,256]{1,0:T(8,128)(2,1)S(1)}, bf16[16,256]{1,0:T(8,128)(2,1)}, u32[]{:S(2)}) copy-start(bf16[16,256]{1,0:T(8,128)(2,1)} %param.22) | copy-start | bytes 24580
  237.2 805.6 %all-to-all-start.4 = ((bf16[128,2,2,12288]{0,2,1,3:T(2,128)(2,1)}), bf16[128,2,2,12288]{0,2,1,3:T(2,128)(2,1)}, u32[]{:S(2)}, u32[]{:S(2)}) async-start(bf16[128,2,2,12288]{0,2,1,3:T(2,128)(2,1)} %copy.92), calls=%async_computation.4 | async-start | bytes 25165824 | tf_op jit(solution)/shard_map/all_to_all | solution.py:65
  243.7 795.9 %all-reduce.4.cloned.1.call-start = ((), (), s32[]{:S(2)}) async-start(), calls=%async_computation.11 | async-start | bytes 131072
  767.6 23.7 %copy-start = (f32[8,16,2048]{2,1,0:T(8,128)S(1)}, f32[8,16,2048]{2,1,0:T(8,128)}, u32[]{:S(2)}) copy-start(f32[8,16,2048]{2,1,0:T(8,128)} %param.17) | copy-start | bytes 3145732
  998.8 10.9 copy-start.8
  1042.8 36.8 %all-to-all-start.3 = ((bf16[4,8,512]{2,0,1:T(4,128)(2,1)}), bf16[4,8,512]{2,0,1:T(4,128)(2,1)S(1)}, u32[]{:S(2)}, u32[]{:S(2)}) async-start(bf16[4,8,512]{2,0,1:T(4,128)(2,1)} %copy.90), calls=%async_computation.3 | async-start | bytes 65536 | tf_op jit(solution)/shard_map/all_to_all | solution.py:155
  1048.3 113.6 %reduce-scatter.2.cloned.1.call-start = ((), (), s32[]{:S(2)}) async-start(), calls=%async_computation.9 | async-start | bytes 1769472 | tf_op jit(solution)/shard_map/reduce_scatter | solution.py:173
  1092.3 3.9 copy-start.6
  1092.3 46.3 %slice-start = ((bf16[3,8,2048]{2,1,0:T(8,128)(2,1)}), bf16[2,8,2048]{2,1,0:T(8,128)(2,1)S(1)}, s32[]{:S(2)}) async-start(bf16[3,8,2048]{2,1,0:T(8,128)(2,1)} %param.16), calls=%async_computation.12 | async-start | bytes 131072 | tf_op jit(solution)/shard_map/slice | solution.py:99
Sparse Core Ops, SparseCore 0:
  29.8 44.7 all-gather.13
  86.8 640.6 all-gather.7
  730.2 40.5 all-gather.9
  772.8 225.9 all-gather.11
  1009.8 29.6 all-reduce.3
  1095.7 66.2 reduce-scatter.1
where the time goes:
time: 1170 us
  blocking collectives  478 us (41%)
  waiting for transfers between devices  399 us (34%)
  local copies, waits for them, and re-layouts  172 us (15%)
  other arithmetic  52.6 us (4%)
  matrix products  34.9 us (3%)
  starting transfers between devices  17.1 us (1%)
  between operations  15.8 us (1%)
    all_gather x1, waiting for transfers between devices, shards(): lax.all_gather(output_blocks, 'rep', axis=1, tiled=True)  206 us
    all_gather x1, blocking collectives, shards(): lax.all_gather(conv_weight, ('rep', 'tp'), axis=1, tiled=True)  179 us
    all_gather x1, waiting for transfers between devices, shards(): shard_piece = lax.all_gather(input_blocks, 'rep', axis=0, tiled=True)  99.1 us
    unnamed x37, local copies, waits for them, and re-layouts  69.4 us
    all_gather x1, blocking collectives, shards(): lax.all_gather(decay_log, ('rep', 'tp'), axis=1, tiled=True)  54.9 us
    all_gather x1, blocking collectives, shards(): lax.all_gather(conv_skip, ('rep', 'tp'), axis=1, tiled=True)  50.8 us
    all_gather x1, blocking collectives, shards(): lax.all_gather(norm_gains, ('rep', 'tp'), axis=1, tiled=True)  49.8 us
    all_to_all x1, waiting for transfers between devices, shards(): lax.all_to_all(input_proj.reshape(model_rows, 1, 2, inner_all), 'tp', spl...  48.1 us
  transfers between devices with their start and end apart: 9, of which 5 were waited for; matrix products, arithmetic and copies ran while one was open for 20% of the time, Pallas kernels for 0%

commit v1 on v0

v1 whole, which is shorter than its diff:
```python
import jax
import jax.numpy as jnp
from jax import lax
from jax.sharding import PartitionSpec as P

CAPACITY = 2
LANES = 128


epsilon = 1e-05


def shards(
    tokens,
    conv_state,
    ssm_state,
    norm_gains,
    conv_weight,
    conv_skip,
    step_bias,
    decay_log,
    input_proj,
    select_proj,
    step_proj,
    output_proj,
    router,
    expert_proj,
    expert_ids,
):
    f32, bf16 = jnp.float32, jnp.bfloat16
    both = ("rep", "tp")
    tp_count = lax.axis_size("tp")
    rep_count = lax.axis_size("rep")
    count = tp_count * rep_count
    tp_index = lax.axis_index("tp")
    rep_index = lax.axis_index("rep")
    tok_dev, width = tokens.shape
    slice_dev = width // count
    token_count = tok_dev * count
    req = tok_dev * tp_count
    inner_all = input_proj.shape[2]
    inner_dev = ssm_state.shape[2]
    state_count = ssm_state.shape[1]
    step_rank = step_proj.shape[0] * count
    expert_total = router.shape[1]
    window_count = expert_proj.shape[1]

    tok = tokens.astype(f32)
    scale = lax.rsqrt(jnp.mean(tok * tok, axis=-1, keepdims=True) + epsilon)
    extra = jnp.concatenate([scale, expert_ids.astype(f32)], axis=1)
    extra = jnp.pad(extra, ((0, 0), (0, LANES - 3)))
    sent = jnp.concatenate(
        [
            tok.reshape(tok_dev, count, slice_dev),
            jnp.broadcast_to(extra[:, None, :], (tok_dev, count, LANES)),
        ],
        axis=2,
    ).transpose(1, 0, 2)
    got = lax.all_to_all(sent, both, split_axis=0, concat_axis=0, tiled=True)
    got = got.reshape(token_count, slice_dev + LANES)
    tok_slice = got[:, :slice_dev]
    scale_all = got[:, slice_dev : slice_dev + 1]
    ids_all = got[:, slice_dev + 1 : slice_dev + 3].astype(jnp.int32)

    gains = norm_gains.astype(f32)
    normed = (tok_slice * scale_all * gains[0]).astype(bf16)
    partial_in = jnp.dot(
        normed, input_proj.reshape(slice_dev, 2 * inner_all), preferred_element_type=f32
    ).astype(bf16)
    partial_in = partial_in.reshape(token_count, 2, inner_all)
    partial_in = lax.psum_scatter(partial_in, "rep", scatter_dimension=0, tiled=True)
    partial_in = lax.psum_scatter(partial_in, "tp", scatter_dimension=2, tiled=True)
    conv_input = partial_in[:, 0].astype(f32)
    gate_z = partial_in[:, 1].astype(f32)

    packed = jnp.concatenate([conv_weight, conv_skip, step_bias[None], decay_log], axis=0)
    packed = lax.all_gather(packed, both, axis=1, tiled=True)
    packed = lax.dynamic_slice_in_dim(packed, tp_index * inner_dev, inner_dev, 1).astype(f32)
    taps = conv_weight.shape[0]
    conv_taps = packed[:taps]
    skip_rows = packed[taps : taps + 2]
    shift_dev = packed[taps + 2]
    decay_dev = packed[taps + 3 :]
    step_rows = lax.all_to_all(
        step_proj.reshape(step_proj.shape[0], tp_count, inner_dev),
        "tp",
        split_axis=1,
        concat_axis=0,
        tiled=True,
    )
    step_rows = lax.all_gather(
        step_rows.reshape(tp_count * step_proj.shape[0], inner_dev), "rep", axis=0, tiled=True
    )
    select_rows = lax.all_gather(select_proj, "rep", axis=1, tiled=True)

    history = conv_state.astype(f32)
    conv_mix = (
        jnp.sum(conv_taps[:-1, None, :] * history, axis=0)
        + conv_taps[-1] * conv_input
        + skip_rows[0]
    )
    conv_next = jnp.concatenate([conv_state[1:], partial_in[:, 0][None]], axis=0)
    activated = jax.nn.silu(conv_mix)
    select_part = jnp.dot(activated.astype(bf16), select_rows, preferred_element_type=f32)
    selected = lax.psum(select_part.astype(bf16), "tp").astype(f32)
    step_low = selected[:, :step_rank].astype(bf16)
    input_map = selected[:, step_rank : step_rank + state_count]
    output_map = selected[:, step_rank + state_count :]
    step_size = jax.nn.softplus(
        jnp.dot(step_low, step_rows, preferred_element_type=f32) + shift_dev
    )
    decay_rate = -jnp.exp(decay_dev)
    factor = jnp.exp(step_size[:, None, :] * decay_rate[None])
    ssm_next = factor * ssm_state + (step_size * activated)[:, None, :] * input_map[:, :, None]
    readout = jnp.sum(ssm_next * output_map[:, :, None], axis=1) + skip_rows[1] * activated
    gated_out = (readout * jax.nn.silu(gate_z)).astype(bf16)

    gated_all = lax.all_gather(gated_out, both, axis=0, tiled=False)
    gated_all = gated_all.reshape(rep_count, tp_count, req, inner_dev)
    gated_all = gated_all.transpose(0, 2, 1, 3).reshape(token_count, inner_all)
    mixer_out = jnp.dot(gated_all, output_proj, preferred_element_type=f32)
    residual = tok_slice + mixer_out
    home = residual.astype(bf16).reshape(count, tok_dev, slice_dev)
    home = lax.all_to_all(home, both, split_axis=0, concat_axis=0, tiled=True)
    mamba_out = home.transpose(1, 0, 2).reshape(tok_dev, width)

    gained = residual * gains[1]
    logit_part = jnp.dot(
        gained, router.astype(f32), preferred_element_type=f32, precision=lax.Precision.HIGHEST
    )
    square_part = jnp.sum(residual * residual, axis=1, keepdims=True)
    summed = lax.psum(jnp.concatenate([logit_part, square_part], axis=1), both)
    scale_two = lax.rsqrt(summed[:, expert_total:] / width + epsilon)
    logits = summed[:, :expert_total] * scale_two
    moe_in = (gained * scale_two).astype(bf16)

    choose = (
        ids_all[:, :, None] == jnp.arange(expert_total, dtype=jnp.int32)[None, None, :]
    ).astype(f32)
    picked = jnp.sum(choose * logits[:, None, :], axis=2)
    first_gate = jax.nn.sigmoid(picked[:, 0] - picked[:, 1])
    second_gate = jax.nn.sigmoid(picked[:, 1] - picked[:, 0])
    window = jnp.arange(window_count, dtype=jnp.int32)
    names_first = ids_all[:, 0:1] == window[None, :]
    names_second = ids_all[:, 1:2] == window[None, :]
    zero = jnp.zeros((), f32)
    gate_w = jnp.where(names_first, first_gate[:, None], zero) + jnp.where(
        names_second, second_gate[:, None], zero
    )
    routed = (names_first | names_second).astype(jnp.int32)
    routed = routed.reshape(count, tok_dev, window_count)
    position = jnp.cumsum(routed, axis=1) - routed
    slot_of = (position[..., None] == jnp.arange(CAPACITY, dtype=jnp.int32)) & (
        routed[..., None] > 0
    )
    slot_of = slot_of.astype(f32)
    blocks_x = moe_in.reshape(count, tok_dev, slice_dev).astype(f32)
    slot_x = jnp.sum(slot_of[..., None] * blocks_x[:, :, None, None, :], axis=1).astype(bf16)
    slot_gate = jnp.sum(slot_of * gate_w.reshape(count, tok_dev, window_count)[..., None], axis=1)
    slot_gate = slot_gate.astype(bf16)

    expert_blocks = lax.all_to_all(expert_proj, "tp", split_axis=3, concat_axis=0, tiled=True)
    hidden_dev = expert_blocks.shape[3]
    slot_rows = lax.all_gather(slot_x, "tp", axis=3, tiled=True)
    product = jnp.einsum(
        "gecd,dexf->gecxf", slot_rows, expert_blocks, preferred_element_type=f32
    ).astype(bf16)
    slot_count = count * window_count * CAPACITY
    summed = lax.psum_scatter(
        product.reshape(slot_count, 2 * hidden_dev), "rep", scatter_dimension=0, tiled=True
    ).astype(f32)
    own = slot_count // rep_count
    gate_own = lax.dynamic_slice_in_dim(slot_gate.reshape(slot_count), rep_index * own, own, 0)
    hidden = (
        gate_own.astype(f32)[:, None]
        * jax.nn.silu(summed[:, :hidden_dev])
        * summed[:, hidden_dev:]
    )
    expert_hidden = hidden.astype(bf16)
    return (mamba_out, conv_next, ssm_next, expert_hidden)


def solution(mesh):
    in_specs = (
        P(("rep", "tp"), None),
        P(None, "rep", "tp"),
        P("rep", None, "tp"),
        P(None, ("rep", "tp")),
        P(None, ("rep", "tp")),
        P(None, ("rep", "tp")),
        P(("rep", "tp")),
        P(None, ("rep", "tp")),
        P(("rep", "tp"), None, None),
        P("tp", "rep"),
        P(("rep", "tp"), None),
        P(None, ("rep", "tp")),
        P(("rep", "tp"), None),
        P(("rep", "tp"), None, None, None),
        P(("rep", "tp"), None),
    )
    out_specs = (P(("rep", "tp"), None), P(None, "rep", "tp"), P("rep", None, "tp"), P("rep", "tp"))
    return jax.shard_map(shards, mesh=mesh, in_specs=in_specs, out_specs=out_specs, check_vma=False)
```

time: 1170 us -> 489 us (0.42)
  blocking collectives: 478 us -> 207 us
  waiting for transfers between devices: 399 us -> 128 us
  local copies, waits for them, and re-layouts: 172 us -> 88.1 us
  other arithmetic: 52.6 us -> 10.6 us
  matrix products: 34.9 us -> 16.5 us
    all_gather x8 -> x2, blocking collectives: 429 us -> 161 us  [the longest x1 155 us: shards(): packed = lax.all_gather(packed, both, axis=1, tiled=True)]
    all_gather x4 -> x3, waiting for transfers between devices: 305 us -> 50.5 us  [the longest x1 50.5 us: shards(): gated_all = lax.all_gather(gated_out, both, axis=0, tiled=False)]
    unnamed x2 -> x0, other arithmetic: 45.4 us -> none
    all_to_all x2 -> x3, waiting for transfers between devices: 48.1 us -> 7.04 us  [the longest x1 7.03 us: shards(): home = lax.all_to_all(home, both, split_axis=0, concat_axis=0, tiled=True)]
    all_gather x1 -> x0, local copies, waits for them, and re-layouts: 40.1 us -> none  [shards(): shard_piece = lax.all_gather(input_blocks, 'rep', axis=0, tiled=True)]
    psum x1 -> x2, blocking collectives: 6.83 us -> 45.7 us  [the longest x1 39.5 us: shards(): summed = lax.psum(jnp.concatenate([logit_part, square_part], axis=1), both)]
    all_to_all x2 -> x0, blocking collectives: 36.2 us -> none  [the longest x1 29.3 us: shards(): lax.all_to_all(output_proj, 'tp', split_axis=0, concat_axis=1, tiled=True)]
    reduce_scatter x1 -> x2, waiting for transfers between devices: 16.7 us -> 52.4 us  [the longest x1 52.4 us: shards(): lax.psum_scatter(product.reshape(slot_count, 2 * hidden_dev), 'rep', scat...]
  transfers between devices with their start and end apart: 9 -> 10, of which waited for: 5 -> 4; matrix products, arithmetic and copies ran while one was open for 20% -> 13% of each run, Pallas kernels for 0% -> 0%
where the time goes in v1:
time: 489 us; the launch traced here: 486 us
  blocking collectives  207 us (42%)
  waiting for transfers between devices  128 us (26%)
  local copies, waits for them, and re-layouts  88.1 us (18%)
  starting transfers between devices  21.1 us (4%)
  matrix products  16.5 us (3%)
  between operations  14.5 us (3%)
  other arithmetic  10.6 us (2%)
    all_gather x1, blocking collectives, shards(): packed = lax.all_gather(packed, both, axis=1, tiled=True)  155 us
    reduce_scatter x1, waiting for transfers between devices, shards(): lax.psum_scatter(product.reshape(slot_count, 2 * hidden_dev), 'rep', scat...  52.4 us
    unnamed x27, local copies, waits for them, and re-layouts  52.4 us
    all_gather x1, waiting for transfers between devices, shards(): gated_all = lax.all_gather(gated_out, both, axis=0, tiled=False)  50.5 us
    psum x1, blocking collectives, shards(): summed = lax.psum(jnp.concatenate([logit_part, square_part], axis=1), both)  39.5 us
    all_to_all x1, local copies, waits for them, and re-layouts, shards(): lax.all_to_all(expert_proj, 'tp', split_axis=3, concat_axis=0, tiled=True)  31.3 us
    unnamed x7, waiting for transfers between devices  18.4 us
  transfers between devices with their start and end apart: 10, of which 4 were waited for; matrix products, arithmetic and copies ran while one was open for 13% of the time, Pallas kernels for 0%

profile of v1, /device:TPU:0, one launch (start us, length us, event | category | flops | bytes accessed | tf_op | source)
XLA Modules:
  0.0 485.9 jit_solution(16441126957380329197)
XLA Ops:
  7.2 1.0 fusion.12
  8.2 0.7 convert_bitcast_fusion
  9.0 0.7 convert_element_type.141
  9.8 0.7 maximum_bitcast_fusion
  10.5 7.3 %all-to-all-start = ((f32[32,2,256]{2,1,0:T(2,128)}), f32[32,2,256]{2,1,0:T(2,128)S(1)}, u32[]{:S(2)}, u32[]{:S(2)}) async-start(f32[32,2,256]{2,1,0:T(2,128)} %maximum_bitcast_fusion), calls=%async_computation | async-start | bytes 131072 | tf_op jit(solution)/shard_map/all_to_all | solution.py:59
  17.8 0.7 convert_element_type.144
  18.5 6.7 %copy.66 = bf16[16,8,2,8192]{3,1,2,0:T(8,128)(2,1)} copy(bf16[16,8,2,8192]{3,2,1,0:T(2,128)(2,1)} %bitcast.102) | data formatting | bytes 8388608
  25.2 0.6 slice_bitcast_fusion.2
  25.9 0.1 slice_reduce_fusion.2
  26.0 4.4 convolution_convert_fusion
  30.4 3.3 all-to-all-start.1
  33.7 41.4 %copy.59 = bf16[128,2,2,12288]{0,2,1,3:T(2,128)(2,1)} copy(bf16[128,2,2,12288]{3,2,1,0:T(2,128)(2,1)} %param.28) | data formatting | bytes 25165824 | tf_op args[13]
  75.2 0.6 copy-done.1
  75.8 6.4 %all-to-all-start.3 = ((bf16[128,2,2,12288]{0,2,1,3:T(2,128)(2,1)}), bf16[128,2,2,12288]{0,2,1,3:T(2,128)(2,1)}, u32[]{:S(2)}, u32[]{:S(2)}) async-start(bf16[128,2,2,12288]{0,2,1,3:T(2,128)(2,1)} %copy.59), calls=%async_computation.4 | async-start | bytes 25165824 | tf_op jit(solution)/shard_map/all_to_all | solution.py:162
  82.2 0.7 all-gather.9.cloned.1.call-update
  83.0 17.2 %reduce-scatter.10.cloned.1.call-done = bf16[8,16384]{1,0:T(8,128)(2,1)} async-done(((bf16[64,16384]{1,0:T(8,128)(2,1)}), bf16[8,16384]{1,0:T(8,128)(2,1)}) %reduce-scatter.10.cloned.1.call-update) | async-done | bytes 262160
  100.4 0.4 all-gather.5.cloned.1.call-update
  100.9 155.0 %all_gather.16 = bf16[23,8192]{1,0:T(8,128)(2,1)S(1)} all-gather(bf16[23,256]{1,0:T(8,128)(2,1)S(1)} %pad_maximum_fusion.1), channel_id=1, replica_groups=mesh['rep'=8,'tp'=4] {'rep','tp'}, dimensions={1}, use_global_device_ids=true | all-gather | bytes 388608 | tf_op jit(solution)/shard_map/all_gather | solution.py:77
  255.9 0.6 fusion.29
  256.6 1.4 reshape.364
  258.0 1.8 convolution_convert_fusion.2
  259.9 6.2 %psum.14 = bf16[8,288]{1,0:T(8,128)(2,1)S(1)} all-reduce(bf16[8,288]{1,0:T(8,128)(2,1)} %convolution_convert_fusion.2), channel_id=1, replica_groups=mesh['rep'=8,'tp'=4] {'tp'}, use_global_device_ids=true, to_apply=%region_4.5 | all-reduce | flops 2304 | bytes 9216 | tf_op jit(solution)/shard_map/psum | solution.py:105
  266.1 1.5 fusion.28
  267.7 2.7 multiply_reduce_fusion
  270.4 0.7 fusion.11
  271.2 0.2 slice_reduce_fusion.1
  271.4 0.1 eq.92
  271.6 0.1 eq.96
  271.8 50.5 %all-gather.7.cloned.1.call-done = bf16[32,8,2048]{2,1,0:T(8,128)(2,1)} async-done(((bf16[1,8,2048]{2,1,0:T(8,128)(2,1)}), bf16[32,8,2048]{2,1,0:T(8,128)(2,1)}) %all-gather.7.cloned.1.call-update) | async-done | bytes 1048592 | tf_op jit(solution)/shard_map/all_gather | solution.py:118
  322.3 1.8 multiply_reduce_fusion.3
  324.1 0.1 fusion.14
  324.3 39.5 %psum.15 = f32[64,17]{0,1:T(8,128)S(1)} all-reduce(f32[64,17]{0,1:T(8,128)S(1)} %pad_maximum_fusion.2), channel_id=1, replica_groups=mesh['rep'=8,'tp'=4] {'rep','tp'}, use_global_device_ids=true, to_apply=%region_8.9 | all-reduce | flops 1088 | bytes 8704 | tf_op jit(solution)/shard_map/psum | solution.py:132
  363.8 0.6 fusion.16
  364.5 6.1 %all_gather.20 = bf16[32,2,2,512]{3,0,2,1:T(8,128)(2,1)S(1)} all-gather(bf16[32,2,2,128]{3,0,2,1:T(8,128)(2,1)S(1)} %multiply_reduce_fusion.2), channel_id=1, replica_groups=mesh['rep'=8,'tp'=4] {'tp'}, dimensions={3}, use_global_device_ids=true | all-gather | bytes 163840 | tf_op jit(solution)/shard_map/all_gather | solution.py:164
  370.6 31.3 %copy.60 = bf16[128,2,2,4,3072]{4,0,3,2,1:T(8,128)(2,1)} copy(bf16[128,2,2,4,3072]{0,2,1,4,3:T(2,128)(2,1)} %bitcast.32) | data formatting | bytes 25165824 | tf_op jit(solution)/shard_map/all_to_all | solution.py:162
  401.8 6.9 %fusion = bf16[32,2,2,2,3072]{4,0,3,2,1:T(8,128)(2,1)S(1)} fusion(bf16[512,2,2,3072,1]{3,0,2,4,1:T(8,128)(2,1)} %bitcast.98, bf16[32,2,2,512]{3,0,2,1:T(8,128)(2,1)S(1)} %all_gather.20), kind=kOutput, calls=%fused_computation.2 | convolution fusion | flops 806092800 | bytes 14286848 | tf_op jit(solution)/shard_map/gecd,dexf->gecxf/dot_general | solution.py:165
  408.7 1.6 copy.61
  410.3 1.5 copy.67
  412.0 0.7 pad_maximum_fusion
  412.9 0.1 broadcast_in_dim.59
  413.1 0.1 copy.57
  413.2 0.1 convert_element_type.160
  413.4 3.8 all-to-all-start.2
  417.3 7.0 %all-to-all-done.2 = bf16[32,2,128]{2,1,0:T(2,128)(2,1)S(1)} async-done(((bf16[32,2,128]{2,1,0:T(2,128)(2,1)}), bf16[32,2,128]{2,1,0:T(2,128)(2,1)S(1)}, u32[]{:S(2)}, u32[]{:S(2)}) %all-to-all-start.2) | async-done | bytes 16416 | tf_op jit(solution)/shard_map/all_to_all | solution.py:124
  424.3 52.4 %reduce-scatter.8.cloned.1.call-done = bf16[16,6144]{1,0:T(8,128)(2,1)} async-done(((bf16[128,6144]{1,0:T(8,128)(2,1)}), bf16[16,6144]{1,0:T(8,128)(2,1)}) %reduce-scatter.8.cloned.1.call-update) | async-done | bytes 196624 | tf_op jit(solution)/shard_map/reduce_scatter | solution.py:169
  476.8 1.0 convert_element_type.169
  477.7 0.7 fusion.1
  478.4 0.6 copy.69
  (72 shorter events, 1.7 us)
Async XLA Ops:
  7.2 315.1 %copy-start = (bf16[8192,128]{1,0:T(8,128)(2,1)S(1)}, bf16[8192,128]{1,0:T(8,128)(2,1)}, u32[]{:S(2)}) copy-start(bf16[8192,128]{1,0:T(8,128)(2,1)} %param.26) | copy-start | bytes 6291460
  10.5 15.3 %all-to-all-start = ((f32[32,2,256]{2,1,0:T(2,128)}), f32[32,2,256]{2,1,0:T(2,128)S(1)}, u32[]{:S(2)}, u32[]{:S(2)}) async-start(f32[32,2,256]{2,1,0:T(2,128)} %maximum_bitcast_fusion), calls=%async_computation | async-start | bytes 131072 | tf_op jit(solution)/shard_map/all_to_all | solution.py:59
  17.8 82.4 %reduce-scatter.10.cloned.1.call-start = ((), (), s32[]{:S(2)}) async-start(), calls=%async_computation.12 | async-start | bytes 2359296
  30.4 44.8 %all-to-all-start.1 = ((bf16[8,4,2048]{2,0,1:T(8,128)(2,1)}), bf16[8,4,2048]{2,0,1:T(8,128)(2,1)S(1)}, u32[]{:S(2)}, u32[]{:S(2)}) async-start(bf16[8,4,2048]{2,0,1:T(8,128)(2,1)} %bitcast.9), calls=%async_computation.2 | async-start | bytes 262144 | tf_op jit(solution)/shard_map/all_to_all | solution.py:84
  75.1 25.2 %copy-start.10 = (bf16[256]{0:T(256)(128)(2,1)S(1)}, bf16[256]{0:T(256)(128)(2,1)}, u32[]{:S(2)}) copy-start(bf16[256]{0:T(256)(128)(2,1)} %param.21) | copy-start | bytes 1540
  75.1 25.2 %copy-start.5 = (bf16[16,256]{1,0:T(8,128)(2,1)S(1)}, bf16[16,256]{1,0:T(8,128)(2,1)}, u32[]{:S(2)}) copy-start(bf16[16,256]{1,0:T(8,128)(2,1)} %param.22) | copy-start | bytes 24580
  75.1 25.2 %copy-start.8 = (bf16[4,256]{1,0:T(4,128)(2,1)S(1)}, bf16[4,256]{1,0:T(4,128)(2,1)}, u32[]{:S(2)}) copy-start(bf16[4,256]{1,0:T(4,128)(2,1)} %param.19) | copy-start | bytes 6148
  75.1 25.2 %copy-start.9 = (bf16[2,256]{1,0:T(2,128)(2,1)S(1)}, bf16[2,256]{1,0:T(2,128)(2,1)}, u32[]{:S(2)}) copy-start(bf16[2,256]{1,0:T(2,128)(2,1)} %param.20) | copy-start | bytes 3076
  75.1 180.7 %copy-start.3 = (bf16[3,8,2048]{2,1,0:T(8,128)(2,1)S(1)}, bf16[3,8,2048]{2,1,0:T(8,128)(2,1)}, u32[]{:S(2)}) copy-start(bf16[3,8,2048]{2,1,0:T(8,128)(2,1)} %param.16) | copy-start | bytes 294916
  75.2 0.7 copy-start.1
  75.8 294.7 %all-to-all-start.3 = ((bf16[128,2,2,12288]{0,2,1,3:T(2,128)(2,1)}), bf16[128,2,2,12288]{0,2,1,3:T(2,128)(2,1)}, u32[]{:S(2)}, u32[]{:S(2)}) async-start(bf16[128,2,2,12288]{0,2,1,3:T(2,128)(2,1)} %copy.59), calls=%async_computation.4 | async-start | bytes 25165824 | tf_op jit(solution)/shard_map/all_to_all | solution.py:162
  82.2 174.4 %all-gather.9.cloned.1.call-start = ((), (), s32[]{:S(2)}) async-start(), calls=%async_computation.11 | async-start | bytes 1474560 | tf_op jit(solution)/shard_map/all_gather | solution.py:94
  82.9 175.1 %reduce-scatter.6.cloned.1.call-start = ((), (), s32[]{:S(2)}) async-start(), calls=%async_computation.7 | async-start | bytes 327680 | tf_op jit(solution)/shard_map/reduce_scatter | solution.py:72
  100.2 165.9 %all-gather.5.cloned.1.call-start = ((), (), s32[]{:S(2)}) async-start(), calls=%async_computation.8 | async-start | bytes 1179648 | tf_op jit(solution)/shard_map/all_gather | solution.py:91
  100.8 221.5 %all-gather.7.cloned.1.call-start = ((), (), s32[]{:S(2)}) async-start(), calls=%async_computation.9 | async-start | bytes 1081344 | tf_op jit(solution)/shard_map/all_gather | solution.py:118
  259.8 10.5 %copy-start.2 = (bf16[8,2,2048]{2,0,1:T(8,128)(2,1)S(1)}, bf16[8,2,2048]{2,0,1:T(8,128)(2,1)}, u32[]{:S(2)}) copy-start(bf16[8,2,2048]{2,0,1:T(8,128)(2,1)} %reduce-scatter.6.cloned.1.call-done) | copy-start | bytes 196612
  259.9 10.5 %copy-start.4 = (f32[1,2048]{1,0:T(1,128)S(1)}, f32[1,2048]{1,0:T(1,128)}, u32[]{:S(2)}) copy-start(f32[1,2048]{1,0:T(1,128)} %get-tuple-element.10) | copy-start | bytes 24580
  270.3 53.8 %copy-start.6 = (f32[128]{0:T(128)S(1)}, f32[128]{0:T(128)}, u32[]{:S(2)}) copy-start(f32[128]{0:T(128)} %get-tuple-element.18) | copy-start | bytes 1540
  270.3 53.8 %copy-start.7 = (bf16[128,16]{0,1:T(8,128)(2,1)S(1)}, bf16[128,16]{0,1:T(8,128)(2,1)}, u32[]{:S(2)}) copy-start(bf16[128,16]{0,1:T(8,128)(2,1)} %param.27) | copy-start | bytes 12292
  271.1 205.7 %reduce-scatter.8.cloned.1.call-start = ((), (), s32[]{:S(2)}) async-start(), calls=%async_computation.10 | async-start | bytes 1769472 | tf_op jit(solution)/shard_map/reduce_scatter | solution.py:169
  410.3 1.7 slice-start
  413.4 11.0 %all-to-all-start.2 = ((bf16[32,2,128]{2,1,0:T(2,128)(2,1)}), bf16[32,2,128]{2,1,0:T(2,128)(2,1)S(1)}, u32[]{:S(2)}, u32[]{:S(2)}) async-start(bf16[32,2,128]{2,1,0:T(2,128)(2,1)} %bitcast.23), calls=%async_computation.3 | async-start | bytes 32768 | tf_op jit(solution)/shard_map/all_to_all | solution.py:124
Sparse Core Ops, SparseCore 0:
  30.5 69.7 reduce-scatter.9
  102.4 40.6 all-gather.8
  145.6 20.3 reduce-scatter.5
  168.5 40.2 all-gather.4
  271.2 51.0 all-gather.6
  412.0 64.6 reduce-scatter.7

commit v2 on v1

--- a/solution.py
+++ b/solution.py
@@ -1,6 +1,10 @@
+import functools
+
 import jax
 import jax.numpy as jnp
 from jax import lax
+from jax.experimental import pallas as pl
+from jax.experimental.pallas import tpu as pltpu
 from jax.sharding import PartitionSpec as P
 
 CAPACITY = 2
@@ -8,6 +12,95 @@
 
 
 epsilon = 1e-05
+MESH = pl.DeviceIdType.MESH
+
+
+def send_kernel(plan, *refs):
+    arrays = len(plan)
+    sources, targets, sems = refs[:arrays], refs[arrays : 2 * arrays], refs[2 * arrays :]
+    barrier = pltpu.get_barrier_semaphore()
+    greeted = 0
+    for axis, count in dict((axis, count) for axis, count, _ in plan).items():
+        me = lax.axis_index(axis)
+        for step in range(1, count):
+            pl.semaphore_signal(
+                barrier, inc=1, device_id={axis: lax.rem(me + step, count)}, device_id_type=MESH
+            )
+        greeted += count - 1
+    pl.semaphore_wait(barrier, greeted)
+    copies = []
+    for which, (axis, count, mode) in enumerate(plan):
+        me = lax.axis_index(axis)
+        for step in range(1, count):
+            peer = lax.rem(me + step, count)
+            source = sources[which]
+            if mode == "lanes":
+                lanes = source.shape[-1] // count
+                source = source.at[:, pl.ds(pl.multiple_of(peer * lanes, lanes), lanes)]
+            elif mode == "lead":
+                source = source.at[peer]
+            copy = pltpu.make_async_remote_copy(
+                src_ref=source,
+                dst_ref=targets[which].at[me],
+                send_sem=sems[2 * which].at[step - 1],
+                recv_sem=sems[2 * which + 1].at[step - 1],
+                device_id={axis: peer},
+                device_id_type=MESH,
+            )
+            copy.start()
+            copies.append(copy)
+    for copy in copies:
+        copy.wait()
+
+
+def send(items, collective_id):
+    shapes, plan, scratch = [], [], []
+    for x, axis, mode in items:
+        count = lax.axis_size(axis)
+        if mode == "lanes":
+            piece = x.shape[:-1] + (x.shape[-1] // count,)
+        elif mode == "lead":
+            piece = x.shape[1:]
+        else:
+            piece = x.shape
+        shapes.append(jax.ShapeDtypeStruct((count,) + piece, x.dtype))
+        plan.append((axis, count, mode))
+        scratch += [pltpu.SemaphoreType.DMA((count - 1,))] * 2
+    return pl.pallas_call(
+        functools.partial(send_kernel, tuple(plan)),
+        out_shape=shapes,
+        in_specs=[pl.BlockSpec(memory_space=pl.ANY)] * len(items),
+        out_specs=[pl.BlockSpec(memory_space=pl.ANY)] * len(items),
+        scratch_shapes=scratch,
+        compiler_params=pltpu.CompilerParams(collective_id=collective_id, has_side_effects=True),
+    )(*[x for x, _, _ in items])
+
+
+def own_piece(x, axis, mode):
+    me = lax.axis_index(axis)
+    if mode == "lanes":
+        lanes = x.shape[-1] // lax.axis_size(axis)
+        return lax.dynamic_slice_in_dim(x, me * lanes, lanes, x.ndim - 1)
+    if mode == "lead":
+        return lax.dynamic_index_in_dim(x, me, 0, keepdims=False)
+    return x
+
+
+def sum_of(item, got):
+    total = own_piece(*item).astype(jnp.float32)
+    me = lax.axis_index(item[1])
+    for sender in range(got.shape[0]):
+        total += jnp.where(me == sender, 0.0, got[sender].astype(jnp.float32))
+    return total
+
+
+def all_of(item, got):
+    return lax.dynamic_update_index_in_dim(got, own_piece(*item), lax.axis_index(item[1]), 0)
+
+
+def gather(x, axis, collective_id):
+    item = (x, axis, "whole")
+    return all_of(item, send([item], collective_id)[0])
 
 
 def shards(
@@ -64,44 +157,60 @@
 
     gains = norm_gains.astype(f32)
     normed = (tok_slice * scale_all * gains[0]).astype(bf16)
+    branches = input_proj.shape[1]
+    diagonal = jnp.eye(branches, dtype=bf16)
+    wide = (diagonal[:, None, None, :] * normed[None, :, :, None]).reshape(
+        branches * token_count, slice_dev * branches
+    )
     partial_in = jnp.dot(
-        normed, input_proj.reshape(slice_dev, 2 * inner_all), preferred_element_type=f32
+        wide, input_proj.reshape(slice_dev * branches, inner_all), preferred_element_type=f32
     ).astype(bf16)
-    partial_in = partial_in.reshape(token_count, 2, inner_all)
-    partial_in = lax.psum_scatter(partial_in, "rep", scatter_dimension=0, tiled=True)
-    partial_in = lax.psum_scatter(partial_in, "tp", scatter_dimension=2, tiled=True)
-    conv_input = partial_in[:, 0].astype(f32)
-    gate_z = partial_in[:, 1].astype(f32)
-
     packed = jnp.concatenate([conv_weight, conv_skip, step_bias[None], decay_log], axis=0)
-    packed = lax.all_gather(packed, both, axis=1, tiled=True)
+    packed_rows = packed.shape[0]
+    packed = jnp.pad(packed, ((0, -packed_rows % 16), (0, 0)))
+    items = [
+        (partial_in, "tp", "lanes"),
+        (packed, "rep", "whole"),
+        (step_proj, "rep", "whole"),
+        (select_proj.T, "rep", "whole"),
+    ]
+    received = send(items, 0)
+    partial_in = sum_of(items[0], received[0])
+    packed, step_rows, select_rows = [
+        all_of(item, got) for item, got in zip(items[1:], received[1:])
+    ]
+    select_rows = select_rows.reshape(-1, inner_dev)
+    partial_in = partial_in.astype(bf16).reshape(branches, rep_count, req, inner_dev)
+    items = [
+        (partial_in[0], "rep", "lead"),
+        (partial_in[1], "rep", "lead"),
+        (packed, "tp", "whole"),
+        (step_rows.reshape(-1, inner_all), "tp", "lanes"),
+    ]
+    received = send(items, 1)
+    conv_input, gate_z = [sum_of(item, got) for item, got in zip(items[:2], received[:2])]
+    packed = all_of(items[2], received[2])
+    packed = packed.transpose(2, 1, 0, 3).reshape(-1, inner_all)[:packed_rows]
+    step_rows = all_of(items[3], received[3])
+    step_rows = step_rows.reshape(tp_count, rep_count, -1, inner_dev)
+    step_rows = step_rows.transpose(1, 0, 2, 3).reshape(step_rank, inner_dev)
     packed = lax.dynamic_slice_in_dim(packed, tp_index * inner_dev, inner_dev, 1).astype(f32)
     taps = conv_weight.shape[0]
     conv_taps = packed[:taps]
     skip_rows = packed[taps : taps + 2]
     shift_dev = packed[taps + 2]
     decay_dev = packed[taps + 3 :]
-    step_rows = lax.all_to_all(
-        step_proj.reshape(step_proj.shape[0], tp_count, inner_dev),
-        "tp",
-        split_axis=1,
-        concat_axis=0,
-        tiled=True,
-    )
-    step_rows = lax.all_gather(
-        step_rows.reshape(tp_count * step_proj.shape[0], inner_dev), "rep", axis=0, tiled=True
-    )
-    select_rows = lax.all_gather(select_proj, "rep", axis=1, tiled=True)
-
     history = conv_state.astype(f32)
     conv_mix = (
         jnp.sum(conv_taps[:-1, None, :] * history, axis=0)
         + conv_taps[-1] * conv_input
         + skip_rows[0]
     )
-    conv_next = jnp.concatenate([conv_state[1:], partial_in[:, 0][None]], axis=0)
+    conv_next = jnp.concatenate([conv_state[1:], conv_input.astype(bf16)[None]], axis=0)
     activated = jax.nn.silu(conv_mix)
-    select_part = jnp.dot(activated.astype(bf16), select_rows, preferred_element_type=f32)
+    select_part = lax.dot_general(
+        activated.astype(bf16), select_rows, (((1,), (1,)), ((), ())), preferred_element_type=f32
+    )
     selected = lax.psum(select_part.astype(bf16), "tp").astype(f32)
     step_low = selected[:, :step_rank].astype(bf16)
     input_map = selected[:, step_rank : step_rank + state_count]
@@ -115,9 +224,9 @@
     readout = jnp.sum(ssm_next * output_map[:, :, None], axis=1) + skip_rows[1] * activated
     gated_out = (readout * jax.nn.silu(gate_z)).astype(bf16)
 
-    gated_all = lax.all_gather(gated_out, both, axis=0, tiled=False)
-    gated_all = gated_all.reshape(rep_count, tp_count, req, inner_dev)
-    gated_all = gated_all.transpose(0, 2, 1, 3).reshape(token_count, inner_all)
+    gated_all = gather(gated_out, "rep", 2).reshape(token_count, inner_dev)
+    gated_all = gather(gated_all, "tp", 3)
+    gated_all = gated_all.transpose(1, 0, 2).reshape(token_count, inner_all)
     mixer_out = jnp.dot(gated_all, output_proj, preferred_element_type=f32)
     residual = tok_slice + mixer_out
     home = residual.astype(bf16).reshape(count, tok_dev, slice_dev)
@@ -129,8 +238,11 @@
         gained, router.astype(f32), preferred_element_type=f32, precision=lax.Precision.HIGHEST
     )
     square_part = jnp.sum(residual * residual, axis=1, keepdims=True)
-    summed = lax.psum(jnp.concatenate([logit_part, square_part], axis=1), both)
-    scale_two = lax.rsqrt(summed[:, expert_total:] / width + epsilon)
+    summed = jnp.concatenate([logit_part, square_part], axis=1)
+    summed = jnp.pad(summed, ((0, 0), (0, LANES - summed.shape[1])))
+    summed = jnp.sum(gather(summed, "tp", 4), axis=0)
+    summed = jnp.sum(gather(summed, "rep", 5), axis=0)
+    scale_two = lax.rsqrt(summed[:, expert_total : expert_total + 1] / width + epsilon)
     logits = summed[:, :expert_total] * scale_two
     moe_in = (gained * scale_two).astype(bf16)
 
@@ -159,22 +271,40 @@
     slot_gate = jnp.sum(slot_of * gate_w.reshape(count, tok_dev, window_count)[..., None], axis=1)
     slot_gate = slot_gate.astype(bf16)
 
-    expert_blocks = lax.all_to_all(expert_proj, "tp", split_axis=3, concat_axis=0, tiled=True)
-    hidden_dev = expert_blocks.shape[3]
-    slot_rows = lax.all_gather(slot_x, "tp", axis=3, tiled=True)
-    product = jnp.einsum(
-        "gecd,dexf->gecxf", slot_rows, expert_blocks, preferred_element_type=f32
+    rows = count * CAPACITY
+    pairs = window_count * 2
+    diagonal = jnp.eye(pairs, dtype=bf16).reshape(window_count, 2, pairs)
+    rows_of = slot_x.transpose(1, 0, 2, 3).reshape(window_count, rows, slice_dev)
+    wide = diagonal[:, :, None, None, :] * rows_of[:, None, :, :, None]
+    partial_up = jnp.dot(
+        wide.reshape(pairs * rows, slice_dev * pairs),
+        expert_proj.reshape(slice_dev * pairs, expert_proj.shape[3]),
+        preferred_element_type=f32,
     ).astype(bf16)
-    slot_count = count * window_count * CAPACITY
-    summed = lax.psum_scatter(
-        product.reshape(slot_count, 2 * hidden_dev), "rep", scatter_dimension=0, tiled=True
-    ).astype(f32)
-    own = slot_count // rep_count
-    gate_own = lax.dynamic_slice_in_dim(slot_gate.reshape(slot_count), rep_index * own, own, 0)
+    hidden_dev = expert_proj.shape[3] // tp_count
+    own = rows // rep_count
+    gate_up, waiting = [], []
+    for expert in range(window_count + 1):
+        items = list(waiting)
+        if expert < window_count:
+            half = partial_up[expert * 2 * rows : (expert + 1) * 2 * rows]
+            items.append((half, "tp", "lanes"))
+        received = send(items, 6 + expert)
+        gate_up += [sum_of(item, got) for item, got in zip(waiting, received)]
+        if expert < window_count:
+            half = sum_of(items[-1], received[-1]).astype(bf16)
+            half = half.reshape(2, rep_count, own, hidden_dev)
+            waiting = [(half[0], "rep", "lead"), (half[1], "rep", "lead")]
+    gate_up = jnp.stack(gate_up).reshape(
+        window_count, 2, own // CAPACITY, CAPACITY, hidden_dev
+    ).transpose(1, 2, 0, 3, 4)
+    gate_up = gate_up.reshape(2, window_count * own, hidden_dev)
+    own_slots = window_count * own
+    gate_own = lax.dynamic_slice_in_dim(slot_gate.reshape(-1), rep_index * own_slots, own_slots, 0)
     hidden = (
         gate_own.astype(f32)[:, None]
-        * jax.nn.silu(summed[:, :hidden_dev])
-        * summed[:, hidden_dev:]
+        * jax.nn.silu(gate_up[0])
+        * gate_up[1]
     )
     expert_hidden = hidden.astype(bf16)
     return (mamba_out, conv_next, ssm_next, expert_hidden)

time: 489 us -> 347 us (0.71)
  Pallas kernels: 0 us -> 212 us
  blocking collectives: 207 us -> 7.95 us
  waiting for transfers between devices: 128 us -> 5.64 us
  local copies, waits for them, and re-layouts: 88.1 us -> 56.9 us
  other arithmetic: 10.6 us -> 33.1 us
  between operations: 14.5 us -> 1.32 us
  starting transfers between devices: 21.1 us -> 12.2 us
    pallas_call x0 -> x9, Pallas kernels: none -> 212 us  [send(): pl.pallas_call(functools.partial(send_kernel, tuple(plan)), out_shape=sha...]
    all_gather x2 -> x0, blocking collectives: 161 us -> none  [the longest x1 155 us: shards(): packed = lax.all_gather(packed, both, axis=1, tiled=True)]
    reduce_scatter x2 -> x0, waiting for transfers between devices: 52.4 us -> none  [the longest x1 52.4 us: shards(): lax.psum_scatter(product.reshape(slot_count, 2 * hidden_dev), 'rep', scat...]
    unnamed x27 -> x58, local copies, waits for them, and re-layouts: 52.4 us -> 0.81 us
    all_gather x3 -> x0, waiting for transfers between devices: 50.5 us -> none  [the longest x1 50.5 us: shards(): gated_all = lax.all_gather(gated_out, both, axis=0, tiled=False)]
    psum x1 -> x0, blocking collectives: 39.5 us -> none  [shards(): summed = lax.psum(jnp.concatenate([logit_part, square_part], axis=1), both)]
    reshape x0 -> x6, local copies, waits for them, and re-layouts: none -> 36.2 us  [the longest x1 25 us: shards(): expert_proj.reshape(slice_dev * pairs, expert_proj.shape[3])]
    all_to_all x1 -> x0, local copies, waits for them, and re-layouts: 31.3 us -> none  [shards(): lax.all_to_all(expert_proj, 'tp', split_axis=3, concat_axis=0, tiled=True)]
  transfers between devices with their start and end apart: 10 -> 2, of which waited for: 4 -> 1; matrix products, arithmetic and copies ran while one was open for 13% -> 10% of each run, Pallas kernels for 0% -> 0%
where the time goes in v2:
time: 347 us; the launch traced here: 345 us
  Pallas kernels  212 us (61%)
  local copies, waits for them, and re-layouts  56.9 us (16%)
  other arithmetic  33.1 us (10%)
  matrix products  15.9 us (5%)
  starting transfers between devices  12.2 us (4%)
  blocking collectives  7.95 us (2%)
  waiting for transfers between devices  5.64 us (2%)
    pallas_call x9, Pallas kernels, send(): pl.pallas_call(functools.partial(send_kernel, tuple(plan)), out_shape=sha...  212 us
    reshape x1, local copies, waits for them, and re-layouts, shards(): expert_proj.reshape(slice_dev * pairs, expert_proj.shape[3])  25 us
    dot_general x1, matrix products, shards(): jnp.dot(wide.reshape(pairs * rows, slice_dev * pairs), expert_proj.reshap...  8.35 us
    psum x1, blocking collectives, shards(): selected = lax.psum(select_part.astype(bf16), 'tp').astype(f32)  7.95 us
    all_to_all x1, starting transfers between devices, shards(): got = lax.all_to_all(sent, both, split_axis=0, concat_axis=0, tiled=True)  7.33 us
    reshape x1, local copies, waits for them, and re-layouts, shards(): input_proj.reshape(slice_dev * branches, inner_all)  7.22 us
  transfers between devices with their start and end apart: 2, of which 1 were waited for; matrix products, arithmetic and copies ran while one was open for 10% of the time, Pallas kernels for 0%

profile of v2, /device:TPU:0, one launch (start us, length us, event | category | flops | bytes accessed | tf_op | source)
XLA Modules:
  0.0 345.0 jit_solution(16532648257033114700)
XLA Ops:
  0.6 1.0 fusion.14
  1.7 0.7 convert_bitcast_fusion
  3.9 7.3 %all-to-all-start = ((f32[32,2,256]{2,1,0:T(2,128)}), f32[32,2,256]{2,1,0:T(2,128)S(1)}, u32[]{:S(2)}, u32[]{:S(2)}) async-start(f32[32,2,256]{2,1,0:T(2,128)} %maximum_bitcast_fusion), calls=%async_computation | async-start | bytes 131072 | tf_op jit(solution)/shard_map/all_to_all | solution.py:152
  13.0 7.2 %reshape.428 = bf16[256,8192]{1,0:T(8,128)(2,1)} reshape(bf16[128,2,8192]{2,1,0:T(2,128)(2,1)} %param.23) | data formatting | bytes 8388608 | tf_op jit(solution)/shard_map/reshape | solution.py:166
  20.3 25.0 %reshape.437 = bf16[512,12288]{1,0:T(8,128)(2,1)} reshape(bf16[128,2,2,12288]{3,2,1,0:T(2,128)(2,1)} %param.28) | data formatting | bytes 25165824 | tf_op jit(solution)/shard_map/reshape | solution.py:281
  46.6 4.3 %convolution_convert_fusion.1.refs_0_ = bf16[128,8192]{1,0:T(8,128)(2,1)} fusion(bf16[128,256]{0,1:T(8,128)(2,1)S(1)} %mul.267, bf16[256,8192]{1,0:T(8,128)(2,1)} %reshape.428), kind=kOutput, calls=%fused_computation.1 | convolution fusion | flops 537919488 | bytes 6356992 | tf_op jit(solution)/shard_map/dot_general | solution.py:165
  50.8 50.4 %shard_map.174 = (bf16[4,128,2048]{2,1,0:T(8,128)(2,1)}, bf16[8,32,256]{2,1,0:T(8,128)(2,1)}, bf16[8,8,8192]{2,1,0:T(8,128)(2,1)}, bf16[8,36,2048]{2,1,0:T(8,128)(2,1)}) custom-call(bf16[128,8192]{1,0:T(8,128)(2,1)} %convolution_convert_fusion.1.refs_0_, bf16[32,256]{1,0:T(8,128)(2,1)} %fusion.30.refs_1_, bf16[8,8192]{1,0:T(8,128)(2,1)} %refs_2_.1, ...), custom_call_target="tpu_custom_call" | custom-call | tf_op jit(solution)/shard_map/pallas_call | solution.py:69
  101.2 2.2 fusion.2
  103.4 0.8 slice_bitcast_fusion.4
  105.5 29.8 %shard_map.175 = (bf16[8,8,2048]{2,1,0:T(8,128)(2,1)}, bf16[8,8,2048]{2,1,0:T(8,128)(2,1)}, bf16[4,8,32,256]{3,2,1,0:T(8,128)(2,1)}, bf16[4,64,2048]{2,1,0:T(8,128)(2,1)}) custom-call(bf16[8,8,2048]{2,1,0:T(8,128)(2,1)} %get-tuple-element.47.refs_0_, bf16[8,8,2048]{2,1,0:T(8,128)(2,1)} %get-tuple-element.46.refs_1_, ...), custom_call_target="tpu_custom_call" | custom-call | tf_op jit(solution)/shard_map/pallas_call | solution.py:69
  136.0 1.1 slice.393
  137.4 1.0 slice.306
  138.4 0.9 dynamic-slice_convert_fusion
  140.6 0.9 slice_convert_fusion
  143.9 1.0 bitcast_dynamic-update-slice_fusion.1
  144.9 1.1 copy.98
  146.7 1.4 reshape.430
  148.1 1.6 fusion.38
  149.7 1.0 convolution_convert_fusion.2
  150.8 8.0 %psum.7 = bf16[8,288]{1,0:T(8,128)(2,1)S(1)} all-reduce(bf16[8,288]{1,0:T(8,128)(2,1)} %convolution_convert_fusion.2), channel_id=1, replica_groups=mesh['rep'=8,'tp'=4] {'tp'}, use_global_device_ids=true, to_apply=%region_2.3 | all-reduce | flops 2304 | bytes 9216 | tf_op jit(solution)/shard_map/psum | solution.py:214
  158.8 1.5 fusion.37
  160.4 1.5 multiply_reduce_fusion
  161.9 1.5 fusion.13
  163.4 8.7 %shard_map.176 = bf16[8,8,2048]{2,1,0:T(8,128)(2,1)} custom-call(bf16[8,2048]{1,0:T(8,128)(2,1)} %get-tuple-element.36.refs_0_), custom_call_target="tpu_custom_call" | custom-call | tf_op jit(solution)/shard_map/pallas_call | solution.py:69
  172.1 1.4 fusion.15
  173.4 12.5 %shard_map.177 = bf16[4,64,2048]{2,1,0:T(8,128)(2,1)} custom-call(bf16[64,2048]{1,0:T(8,128)(2,1)} %bitcast.181), custom_call_target="tpu_custom_call" | custom-call | tf_op jit(solution)/shard_map/pallas_call | solution.py:69
  186.0 1.7 bitcast_dynamic-update-slice_fusion
  187.7 1.3 copy.115
  190.6 5.9 %shard_map.178 = f32[4,64,128]{2,1,0:T(8,128)} custom-call(f32[64,128]{1,0:T(8,128)} %pad.14.refs_0_), custom_call_target="tpu_custom_call" | custom-call | tf_op jit(solution)/shard_map/pallas_call | solution.py:69
  197.1 1.5 reduce_sum.91.refs_0_
  198.7 9.2 %shard_map.179 = f32[8,64,128]{2,1,0:T(8,128)} custom-call(f32[64,128]{1,0:T(8,128)} %reduce_sum.91.refs_0_), custom_call_target="tpu_custom_call" | custom-call | tf_op jit(solution)/shard_map/pallas_call | solution.py:69
  207.9 1.4 bitcast_dynamic-update-slice_fusion.5
  209.3 1.0 reduce_sum.92
  213.0 8.3 %convolution_convert_fusion = bf16[256,12288]{1,0:T(8,128)(2,1)S(1)} fusion(bf16[256,512]{0,1:T(8,128)(2,1)S(1)} %mul.319, bf16[512,12288]{1,0:T(8,128)(2,1)} %reshape.437), kind=kOutput, calls=%fused_computation | convolution fusion | flops 3224371200 | bytes 19136512 | tf_op jit(solution)/shard_map/dot_general | solution.py:279
  221.4 3.1 fusion.39
  224.4 35.3 %shard_map.180 = bf16[4,128,3072]{2,1,0:T(8,128)(2,1)} custom-call(bf16[128,12288]{1,0:T(8,128)(2,1)} %get-tuple-element.41.refs_0_), custom_call_target="tpu_custom_call" | custom-call | tf_op jit(solution)/shard_map/pallas_call | solution.py:69
  259.7 2.8 fusion.1
  262.5 0.9 slice_bitcast_fusion.2
  263.5 40.4 %shard_map.181 = (bf16[8,8,3072]{2,1,0:T(8,128)(2,1)}, bf16[8,8,3072]{2,1,0:T(8,128)(2,1)}, bf16[4,128,3072]{2,1,0:T(8,128)(2,1)}) custom-call(bf16[8,8,3072]{2,1,0:T(8,128)(2,1)} %get-tuple-element.45.refs_0_, bf16[8,8,3072]{2,1,0:T(8,128)(2,1)} %get-tuple-element.44.refs_1_, bf16[128,12288]{1,0:T(8,128)(2,1)} %get-tuple-element.40.refs_2_), custom_call_target="tpu_custom_call" | custom-call | tf_op jit(solution)/shard_map/pallas_call | solution.py:69
  303.9 1.1 select_add_fusion.3
  305.0 1.1 select_add_fusion.2
  306.1 2.8 fusion
  308.9 0.9 slice_bitcast_fusion
  309.8 19.8 %shard_map.182 = (bf16[8,8,3072]{2,1,0:T(8,128)(2,1)}, bf16[8,8,3072]{2,1,0:T(8,128)(2,1)}) custom-call(bf16[8,8,3072]{2,1,0:T(8,128)(2,1)} %get-tuple-element.43.refs_0_, bf16[8,8,3072]{2,1,0:T(8,128)(2,1)} %get-tuple-element.42.refs_1_), custom_call_target="tpu_custom_call" | custom-call | tf_op jit(solution)/shard_map/pallas_call | solution.py:69
  329.6 1.1 select_add_fusion.1
  330.7 1.1 select_add_fusion
  332.4 4.9 %all-to-all-start.1 = ((bf16[32,2,128]{2,1,0:T(2,128)(2,1)}), bf16[32,2,128]{2,1,0:T(2,128)(2,1)S(1)}, u32[]{:S(2)}, u32[]{:S(2)}) async-start(bf16[32,2,128]{2,1,0:T(2,128)(2,1)} %bitcast.33), calls=%async_computation.1 | async-start | bytes 32768 | tf_op jit(solution)/shard_map/all_to_all | solution.py:233
  338.8 5.6 %all-to-all-done.1 = bf16[32,2,128]{2,1,0:T(2,128)(2,1)S(1)} async-done(((bf16[32,2,128]{2,1,0:T(2,128)(2,1)}), bf16[32,2,128]{2,1,0:T(2,128)(2,1)S(1)}, u32[]{:S(2)}, u32[]{:S(2)}) %all-to-all-start.1) | async-done | bytes 16416 | tf_op jit(solution)/shard_map/all_to_all | solution.py:233
  (134 shorter events, 18.8 us)
Async XLA Ops:
  0.6 188.4 %copy-start = (bf16[8192,128]{1,0:T(8,128)(2,1)S(1)}, bf16[8192,128]{1,0:T(8,128)(2,1)}, u32[]{:S(2)}) copy-start(bf16[8192,128]{1,0:T(8,128)(2,1)} %param.26) | copy-start | bytes 6291460
  3.9 41.9 %all-to-all-start = ((f32[32,2,256]{2,1,0:T(2,128)}), f32[32,2,256]{2,1,0:T(2,128)S(1)}, u32[]{:S(2)}, u32[]{:S(2)}) async-start(f32[32,2,256]{2,1,0:T(2,128)} %maximum_bitcast_fusion), calls=%async_computation | async-start | bytes 131072 | tf_op jit(solution)/shard_map/all_to_all | solution.py:152
  13.0 7.2 %copy-start.27 = (bf16[256]{0:T(256)(128)(2,1)S(1)}, bf16[256]{0:T(256)(128)(2,1)}, u32[]{:S(2)}) copy-start(bf16[256]{0:T(256)(128)(2,1)} %param.21) | copy-start | bytes 1540
  20.2 25.0 %copy-start.14 = (bf16[16,256]{1,0:T(8,128)(2,1)S(1)}, bf16[16,256]{1,0:T(8,128)(2,1)}, u32[]{:S(2)}) copy-start(bf16[16,256]{1,0:T(8,128)(2,1)} %param.22) | copy-start | bytes 24580
  20.2 25.0 %copy-start.22 = (bf16[4,256]{1,0:T(4,128)(2,1)S(1)}, bf16[4,256]{1,0:T(4,128)(2,1)}, u32[]{:S(2)}) copy-start(bf16[4,256]{1,0:T(4,128)(2,1)} %param.19) | copy-start | bytes 6148
  20.3 25.0 %copy-start.25 = (bf16[2,256]{1,0:T(2,128)(2,1)S(1)}, bf16[2,256]{1,0:T(2,128)(2,1)}, u32[]{:S(2)}) copy-start(bf16[2,256]{1,0:T(2,128)(2,1)} %param.20) | copy-start | bytes 3076
  45.9 4.9 %copy-start.5 = (f32[64,256]{1,0:T(8,128)}, f32[64,256]{1,0:T(8,128)S(1)}, u32[]{:S(2)}) copy-start(f32[64,256]{1,0:T(8,128)S(1)} %reshape.427) | copy-start | bytes 196612
  101.2 3.6 %copy-start.7 = (bf16[8,8192]{1,0:T(8,128)(2,1)S(1)}, bf16[8,8192]{1,0:T(8,128)(2,1)}, u32[]{:S(2)}) copy-start(bf16[8,8192]{1,0:T(8,128)(2,1)} %refs_2_.1) | copy-start | bytes 393220
  104.9 30.5 %copy-start.9 = (bf16[8,32,256]{2,1,0:T(8,128)(2,1)S(1)}, bf16[8,32,256]{2,1,0:T(8,128)(2,1)}, u32[]{:S(2)}) copy-start(bf16[8,32,256]{2,1,0:T(8,128)(2,1)} %bitcast_dynamic-update-slice_fusion.7.refs_2_) | copy-start | bytes 393220
  136.0 7.9 %copy-start.3 = (bf16[4,64,2048]{2,1,0:T(8,128)(2,1)S(1)}, bf16[4,64,2048]{2,1,0:T(8,128)(2,1)}, u32[]{:S(2)}) copy-start(bf16[4,64,2048]{2,1,0:T(8,128)(2,1)} %get-tuple-element.23) | copy-start | bytes 3145732
  139.9 6.0 %copy-start.10 = (bf16[3,8,2048]{2,1,0:T(8,128)(2,1)S(1)}, bf16[3,8,2048]{2,1,0:T(8,128)(2,1)}, u32[]{:S(2)}) copy-start(bf16[3,8,2048]{2,1,0:T(8,128)(2,1)} %param.16) | copy-start | bytes 294916
  140.6 5.4 %copy-start.4 = (bf16[2048,36]{0,1:T(8,128)(2,1)S(1)}, bf16[2048,36]{0,1:T(8,128)(2,1)}, u32[]{:S(2)}) copy-start(bf16[2048,36]{0,1:T(8,128)(2,1)} %param.24) | copy-start | bytes 442372
  142.5 3.5 %copy-start.16 = (s32[32,2]{0,1:T(2,128)}, s32[32,2]{0,1:T(2,128)S(1)}, u32[]{:S(2)}) copy-start(s32[32,2]{0,1:T(2,128)S(1)} %copy.101) | copy-start | bytes 772
  142.7 3.3 copy-start.18
  148.1 12.2 %copy-start.8 = (f32[16,2048]{1,0:T(8,128)S(1)}, f32[16,2048]{1,0:T(8,128)}, u32[]{:S(2)}) copy-start(f32[16,2048]{1,0:T(8,128)} %fusion.3) | copy-start | bytes 393220
  150.8 9.6 %copy-start.2 = (f32[8,16,2048]{2,1,0:T(8,128)S(1)}, f32[8,16,2048]{2,1,0:T(8,128)}, u32[]{:S(2)}) copy-start(f32[8,16,2048]{2,1,0:T(8,128)} %param.17) | copy-start | bytes 3145732
  158.8 3.1 copy-start.11
  158.8 3.1 copy-start.13
  186.0 3.0 copy-start.6
  189.0 0.7 copy-start.23
  189.0 0.7 copy-start.24
  189.0 22.1 %copy-start.26 = (s32[64,2]{0,1:T(2,128)S(1)}, s32[64,2]{0,1:T(2,128)}, u32[]{:S(2)}) copy-start(s32[64,2]{0,1:T(2,128)} %copy.103) | copy-start | bytes 1540
  189.0 22.5 %copy-start.17 = (s32[32,2]{0,1:T(2,128)S(1)}, s32[32,2]{0,1:T(2,128)}, u32[]{:S(2)}) copy-start(s32[32,2]{0,1:T(2,128)} %copy-done.16) | copy-start | bytes 772
  189.0 22.5 %copy-start.19 = (s32[32,2]{0,1:T(2,128)S(1)}, s32[32,2]{0,1:T(2,128)}, u32[]{:S(2)}) copy-start(s32[32,2]{0,1:T(2,128)} %copy-done.18) | copy-start | bytes 772
  189.1 22.5 %copy-start.15 = (s32[32,2,2]{0,2,1:T(2,128)S(1)}, s32[32,2,2]{0,2,1:T(2,128)}, u32[]{:S(2)}) copy-start(s32[32,2,2]{0,2,1:T(2,128)} %reduce-window_subtract_fusion) | copy-start | bytes 1540
  189.1 22.5 %copy-start.20 = (pred[32,2,2]{0,2,1:T(4,128)(4,1)S(1)}, pred[32,2,2]{0,2,1:T(4,128)(4,1)}, u32[]{:S(2)}) copy-start(pred[32,2,2]{0,2,1:T(4,128)(4,1)} %fusion.34) | copy-start | bytes 388
  189.7 22.5 %copy-start.21 = (bf16[2,2,4]{1,0,2:T(2,128)(2,1)S(1)}, bf16[2,2,4]{1,0,2:T(2,128)(2,1)}, u32[]{:S(2)}) copy-start(bf16[2,2,4]{1,0,2:T(2,128)(2,1)} %compare_convert_fusion) | copy-start | bytes 100
  331.8 13.3 %copy-start.1 = (bf16[8192,128]{1,0:T(8,128)(2,1)S(1)}, bf16[8192,128]{1,0:T(8,128)(2,1)}, u32[]{:S(2)}) copy-start(bf16[8192,128]{1,0:T(8,128)(2,1)} %param.26) | copy-start | bytes 6291460
  332.0 6.1 %slice-start = ((bf16[3,8,2048]{2,1,0:T(8,128)(2,1)}), bf16[2,8,2048]{2,1,0:T(8,128)(2,1)S(1)}, s32[]{:S(2)}) async-start(bf16[3,8,2048]{2,1,0:T(8,128)(2,1)} %param.16), calls=%async_computation.2 | async-start | bytes 131072 | tf_op jit(solution)/shard_map/slice | solution.py:209
  332.0 6.1 %copy-start.12 = (bf16[1,8,2048]{2,1,0:T(8,128)(2,1)S(1)}, bf16[1,8,2048]{2,1,0:T(8,128)(2,1)}, u32[]{:S(2)}) copy-start(bf16[1,8,2048]{2,1,0:T(8,128)(2,1)} %get-tuple-element.34) | copy-start | bytes 98308
  332.4 12.0 %all-to-all-start.1 = ((bf16[32,2,128]{2,1,0:T(2,128)(2,1)}), bf16[32,2,128]{2,1,0:T(2,128)(2,1)S(1)}, u32[]{:S(2)}, u32[]{:S(2)}) async-start(bf16[32,2,128]{2,1,0:T(2,128)(2,1)} %bitcast.33), calls=%async_computation.1 | async-start | bytes 32768 | tf_op jit(solution)/shard_map/all_to_all | solution.py:233
